TPU v7x, 32 devices: a whole 2x2x4 slice. The times are simulated.
32 devices in a mesh: dp: 4 (over x, y), tp: 8 (over z, core).
Axes of the slice: x: 2, y: 2, z: 4, core: 2. Of those that a mesh axis runs over, the one named last changes fastest.
Arguments:
- x: bfloat16 [8192, 5120], P('dp'), parts along dimension 0
- dy: bfloat16 [8192, 5120], P('dp'), parts along dimension 0
- gate: bfloat16 [8192, 14336], P('dp', 'tp'), parts along dimension 0
- up: bfloat16 [8192, 14336], P('dp', 'tp'), parts along dimension 0
- w_gate: bfloat16 [5120, 14336], P(None, 'tp')
- w_up: bfloat16 [5120, 14336], P(None, 'tp')
- w_down: bfloat16 [14336, 5120], P('tp')
Outputs:
- output 1: bfloat16 [8192, 5120], P('dp'), parts along dimension 0
- output 2: bfloat16 [20480, 14336], P('dp', 'tp'), parts along dimension 0
- output 3: bfloat16 [20480, 14336], P('dp', 'tp'), parts along dimension 0
- output 4: bfloat16 [57344, 5120], P(('dp', 'tp')), parts along dimension 0
There are 4 independent parts. A program takes and returns all parts, laid end to end along the dimension named above; an argument that names none is the same for every part.
All inputs are finite; a program needn't handle non-finite values.
Results may differ from a plain program's by a relative error of at most 0.012.
Values are sent between devices in bfloat16 or wider.
A program may use at most 2 GiB of HBM per device.

v0:
```python
import jax
import jax.numpy as jnp
from jax import lax
from jax.sharding import PartitionSpec as P


def act(gate, up):
    return jax.nn.silu(gate) * up


def solution(mesh):
    def step(x, dy, gate, up, w_gate, w_up, w_down):
        hidden, back = jax.vjp(act, gate.astype(jnp.float32), up.astype(jnp.float32))
        d_hidden = jnp.dot(dy, w_down.T, preferred_element_type=jnp.float32)
        d_gate, d_up = (g.astype(jnp.bfloat16) for g in back(d_hidden))
        term = jnp.dot(d_gate, w_gate.T, preferred_element_type=jnp.float32) + jnp.dot(d_up, w_up.T, preferred_element_type=jnp.float32)
        dx = lax.psum(term.astype(jnp.bfloat16), "tp")
        dw_gate = jnp.dot(x.T, d_gate, preferred_element_type=jnp.float32)
        dw_up = jnp.dot(x.T, d_up, preferred_element_type=jnp.float32)
        dw_down = jnp.dot(hidden.astype(jnp.bfloat16).T, dy, preferred_element_type=jnp.float32)
        return dx, *(g.astype(jnp.bfloat16) for g in (dw_gate, dw_up, dw_down))

    tokens, columns, rows = P("dp", None), P(None, "tp"), P("tp", None)
    return jax.shard_map(
        step,
        mesh=mesh,
        in_specs=(tokens, tokens, P("dp", "tp"), P("dp", "tp"), columns, columns, rows),
        out_specs=(tokens, P("dp", "tp"), P("dp", "tp"), P(("dp", "tp"), None)),
        check_vma=False,
    )
```

profile of v0, /device:TPU:0, one launch (start us, length us, event | category | flops | bytes accessed | tf_op | source)
XLA Modules:
  0.0 618.7 jit_solution(2766093190700886483)
XLA Ops:
  7.2 0.0 all-reduce.2.cloned.1.call-start
  7.2 56.6 %fusion.8 = (bf16[2048,1792]{1,0:T(8,128)(2,1)S(1)}, f32[2048,1792]{1,0:T(8,128)}) fusion(bf16[2048,1792]{1,0:T(8,128)(2,1)} %param.9, bf16[2048,1792]{1,0:T(8,128)(2,1)} %param.10, bf16[2048,5120]{1,0:T(8,128)(2,1)} %param.8, bf16[1792,5120]{1,0:T(8,128)(2,1)} %param.13), kind=kOutput, calls=%fused_computation.18 | convolution fusion | flops 37628674048 | bytes 76021760 | tf_op jit(solution)/shard_map/dot_general | solution.py:14
  63.8 0.0 copy-start
  63.8 49.0 %fusion.11 = f32[2048,5120]{1,0:T(8,128)} fusion(bf16[2048,1792]{1,0:T(8,128)(2,1)S(1)} %get-tuple-element.8, bf16[5120,1792]{1,0:T(8,128)(2,1)} %param.11), kind=kOutput, calls=%fused_computation.21 | convolution fusion | flops 37580963840 | bytes 67633152 | tf_op jit(solution)/shard_map/dot_general | solution.py:16
  112.9 0.0 copy-done
  112.9 66.8 %add_convert_fusion = bf16[2048,5120]{1,0:T(8,128)(2,1)} fusion(f32[2048,5120]{1,0:T(8,128)} %fusion.11, bf16[5120,1792]{1,0:T(8,128)(2,1)} %param.12, f32[2048,1792]{1,0:T(8,128)} %get-tuple-element.9, bf16[2048,1792]{1,0:T(8,128)(2,1)} %param.9), kind=kOutput, calls=%fused_computation | convolution fusion | flops 37627625472 | bytes 103284736 | tf_op jit(solution)/shard_map/dot_general | solution.py:16
  179.7 0.0 slice-start
  179.7 0.0 all-reduce.2.cloned.1.call-update
  179.7 0.0 slice-start.1
  179.7 52.1 %fusion.1 = bf16[5120,1792]{0,1:T(8,128)(2,1)} fusion(bf16[2048,5120]{1,0:T(8,128)(2,1)} %param.7, f32[2048,1792]{1,0:T(8,128)} %get-tuple-element.9, bf16[2048,1792]{1,0:T(8,128)(2,1)} %param.9), kind=kOutput, calls=%fused_computation.11 | convolution fusion | flops 37615828992 | bytes 61341696 | tf_op jit(solution)/shard_map/dot_general | solution.py:19
  231.8 0.0 slice-done
  231.8 0.0 slice-done.1
  231.8 43.5 %fusion = bf16[5120,1792]{0,1:T(8,128)(2,1)} fusion(bf16[2048,1792]{1,0:T(8,128)(2,1)S(1)} %bitcast.15, bf16[2048,5120]{1,0:T(8,128)(2,1)} %param.7), kind=kOutput, calls=%fused_computation.10 | convolution fusion | flops 37590138880 | bytes 46661632 | tf_op jit(solution)/shard_map/dot_general | solution.py:18
  275.3 23.2 %copy.11 = bf16[5120,1792]{1,0:T(8,128)(2,1)} copy(bf16[5120,1792]{0,1:T(8,128)(2,1)} %fusion) | data formatting | bytes 36700160
  298.5 23.2 %copy.12 = bf16[5120,1792]{1,0:T(8,128)(2,1)} copy(bf16[5120,1792]{0,1:T(8,128)(2,1)} %fusion.1) | data formatting | bytes 36700160
  321.7 59.8 %convolution_convert_fusion = bf16[1792,5120]{1,0:T(8,128)(2,1)} fusion(bf16[2048,5120]{1,0:T(8,128)(2,1)} %param.8, bf16[2048,1792]{1,0:T(8,128)(2,1)} %param.10, bf16[2048,1792]{1,0:T(8,128)(2,1)} %param.9), kind=kOutput, calls=%fused_computation.5 | convolution fusion | flops 37619499008 | bytes 54001664 | tf_op jit(solution)/shard_map/dot_general | solution.py:20
  381.4 212.6 %all-reduce.2.cloned.1.call-done = bf16[2048,5120]{1,0:T(8,128)(2,1)} async-done(((bf16[2048,5120]{1,0:T(8,128)(2,1)}), bf16[2048,5120]{1,0:T(8,128)(2,1)}) %all-reduce.2.cloned.1.call-update) | async-done | bytes 20971536 | tf_op jit(solution)/shard_map/psum | solution.py:17
  594.1 17.3 %copy.14 = bf16[2048,5120]{1,0:T(8,128)(2,1)} copy(bf16[2048,5120]{1,0:T(8,128)(2,1)} %all-reduce.2.cloned.1.call-done) | data formatting | bytes 41943040
  (1 shorter events, 0.0 us)
Async XLA Ops:
  7.2 586.9 %all-reduce.2.cloned.1.call-start = ((), (), s32[]{:S(2)}) async-start(), calls=%async_computation | async-start | bytes 41943040 | tf_op jit(solution)/shard_map/psum | solution.py:17
  63.8 49.0 %copy-start = (bf16[2048,1792]{1,0:T(8,128)(2,1)}, bf16[2048,1792]{1,0:T(8,128)(2,1)S(1)}, u32[]{:S(2)}) copy-start(bf16[2048,1792]{1,0:T(8,128)(2,1)S(1)} %get-tuple-element.8) | copy-start | bytes 22020100
  179.7 52.1 %slice-start = ((s8[7340032]{0:T(1024)(128)(4,1)}), s8[3145728]{0:T(1024)(128)(4,1)S(1)}, s32[]{:S(2)}) async-start(s8[7340032]{0:T(1024)(128)(4,1)} %bitcast.14), calls=%async_computation.1 | async-start | bytes 6291456
  179.7 52.1 %slice-start.1 = ((s8[7340032]{0:T(1024)(128)(4,1)}), s8[4194304]{0:T(1024)(128)(4,1)S(1)}, s32[]{:S(2)}) async-start(s8[7340032]{0:T(1024)(128)(4,1)} %bitcast.14), calls=%async_computation.2 | async-start | bytes 8388608
Sparse Core Ops, SparseCore 0:
  179.8 414.1 all-reduce.1
where the time goes:
time: 625 us; the launch traced here: 619 us
  matrix products  328 us (52%)
  waiting for transfers between devices  213 us (34%)
  local copies, waits for them, and re-layouts  63.6 us (10%)
  between operations  14.6 us (2%)
    psum x1, waiting for transfers between devices, step(): dx = lax.psum(term.astype(jnp.bfloat16), 'tp')  213 us
    dot_general x1, matrix products, step(): jnp.dot(d_up, w_up.T, preferred_element_type=jnp.float32)  66.8 us
    unnamed x9, local copies, waits for them, and re-layouts  63.6 us
    dot_general x1, matrix products, step(): jnp.dot(hidden.astype(jnp.bfloat16).T, dy, preferred_element_type=jnp.flo...  59.8 us
    dot_general x1, matrix products, step(): d_hidden = jnp.dot(dy, w_down.T, preferred_element_type=jnp.float32)  56.6 us
    dot_general x1, matrix products, step(): dw_up = jnp.dot(x.T, d_up, preferred_element_type=jnp.float32)  52.1 us
    dot_general x1, matrix products, step(): jnp.dot(d_gate, w_gate.T, preferred_element_type=jnp.float32)  49 us
    dot_general x1, matrix products, step(): dw_gate = jnp.dot(x.T, d_gate, preferred_element_type=jnp.float32)  43.5 us
  transfers between devices with their start and end apart: 1, of which 1 were waited for; matrix products, arithmetic and copies ran while one was open for 33% of the time, Pallas kernels for 0%

commit v1 on v0

v1 whole, which is shorter than its diff:
```python
import functools

import jax
import jax.numpy as jnp
from jax import lax
from jax.experimental import pallas as pl
from jax.experimental.pallas import tpu as pltpu
from jax.sharding import PartitionSpec as P

BF, F32 = jnp.bfloat16, jnp.float32
MESH = pl.DeviceIdType.MESH
BLOCKS, JT, NT, XT = 4, 7, 10, 10
UNITS = BLOCKS * NT
RING, HOP = 8, 2


def dot(a, b, ca, cb):
    return lax.dot_general(a, b, (((ca,), (cb,)), ((), ())), preferred_element_type=F32)


def kernel(
    x, dy, gate, up, wg, wu, wd,
    dx, dwg, dwu, dwd, chip16, chip32,
    dg_all, du_all, hid_all, dyb, wdb, gb, ub, wgb, wub, xd, og, ou, od,
    tsend, xrecv, own, cst, abuf, bbuf, dbuf, fbuf, cfb,
    s_dy, s_wd, s_g, s_u, s_wg, s_wu, s_xd, s_og, s_ou, s_od,
    x_send, x_recv, s_c, s_cf, a_send, a_recv, b_send, b_recv, f_send, f_recv, p_send, p_recv, s_l,
):
    rb, cb = dyb.shape[0], wgb.shape[1]
    hb = rb // 2
    jb = wdb.shape[1]
    xb = xd.shape[2]
    ib = og.shape[1]
    t = lax.axis_index("tp")
    z, c = t // 2, lax.rem(t, 2)
    inner = jnp.logical_or(z == 1, z == 2)
    outer = jnp.logical_not(inner)
    partner = 2 * z + (1 - c)
    beside = 2 * (z + 1 - 2 * lax.rem(z, 2)) + c
    across = 2 * (3 - z) + c

    barrier = pltpu.get_barrier_semaphore()
    for to in (partner, beside):
        pl.semaphore_signal(barrier, inc=1, device_id={"tp": to}, device_id_type=MESH)

    @pl.when(inner)
    def _():
        pl.semaphore_signal(barrier, inc=1, device_id={"tp": across}, device_id_type=MESH)
        pl.semaphore_wait(barrier, 3)

    @pl.when(outer)
    def _():
        pl.semaphore_wait(barrier, 2)

    def local(src, dst, sem):
        return pltpu.make_async_copy(src, dst, sem)

    def remote(src, dst, send, recv, to):
        return pltpu.make_async_remote_copy(
            src_ref=src, dst_ref=dst, send_sem=send, recv_sem=recv, device_id={"tp": to}, device_id_type=MESH
        )

    def ds(i, n):
        return pl.ds(pl.multiple_of(i * n, n), n)

    def load_dy(b):
        return local(dy.at[ds(b, rb), :], dyb, s_dy)

    def load_hidden(g):
        b, j, s = g // JT, lax.rem(g, JT), lax.rem(g, 2)
        return (
            local(wd.at[ds(j, jb), :], wdb.at[s], s_wd.at[s]),
            local(gate.at[ds(b, rb), ds(j, jb)], gb.at[s], s_g.at[s]),
            local(up.at[ds(b, rb), ds(j, jb)], ub.at[s], s_u.at[s]),
        )

    def load_weights(u):
        n, s = lax.rem(u, NT), lax.rem(u, 2)
        return (
            local(wg.at[ds(n, cb), :], wgb.at[s], s_wg.at[s]),
            local(wu.at[ds(n, cb), :], wub.at[s], s_wu.at[s]),
        )

    def load_x(m, s):
        return local(x.at[:, ds(m, xb)], xd.at[s], s_xd.at[s])

    def load_dyt(m, s):
        return local(dy.at[:, ds(m, xb)], xd.at[s], s_xd.at[s])

    def start(copies):
        for copy in copies:
            copy.start()

    def wait(copies):
        for copy in copies:
            copy.wait()

    def part(u, half):
        b, n = u // NT, lax.rem(u, NT)
        return dx.at[ds(2 * b + half, hb), ds(n, cb)]

    def copy_x(u):
        s = lax.rem(u, 4)
        return remote(tsend.at[s], xrecv.at[s], x_send.at[s], x_recv.at[s], partner)

    def copy_c16(u):
        s = lax.rem(u, 2)
        return local(cst.at[s], chip16.at[u], s_c.at[s])

    def copy_c32(u):
        return local(own.at[lax.rem(u, 4)], chip32.at[u], s_c.at[lax.rem(u, 2)])

    def load_c32(u):
        s = lax.rem(u, 2)
        return local(chip32.at[u], cfb.at[s], s_cf.at[s])

    def copy_a(u):
        s = lax.rem(u, RING)
        return remote(chip16.at[u], abuf.at[s], a_send.at[s], a_recv.at[s], beside)

    def copy_b(u):
        s = lax.rem(u, RING)
        return remote(dbuf.at[s], bbuf.at[s], b_send.at[s], b_recv.at[s], across)

    def copy_f(u):
        return remote(fbuf.at[lax.rem(u, 4)], part(u, c), f_send.at[lax.rem(u, 4)], f_recv.at[u], beside)

    def copy_p_inner(u):
        return remote(fbuf.at[lax.rem(u, 4)], part(u, c), p_send.at[lax.rem(u, 4)], p_recv.at[u], partner)

    def copy_p_outer(u):
        return remote(part(u, c), part(u, c), p_send.at[lax.rem(u, 4)], p_recv.at[u], partner)

    def copy_l(u):
        return local(fbuf.at[lax.rem(u, 4)], part(u, c), s_l.at[lax.rem(u, 4)])

    def chip_sum(u):
        copy_x(u).wait_recv()
        s, o = lax.rem(u, 4), lax.rem(u, 4)
        total = own[o] + xrecv[s].astype(F32)

        @pl.when(outer)
        def _():
            cst[lax.rem(u, 2)] = total.astype(BF)
            copy_c16(u).start()

            @pl.when(u >= 1)
            def _():
                copy_c16(u - 1).wait()

        @pl.when(inner)
        def _():
            own[o] = total
            copy_c32(u).start()

            @pl.when(u >= 1)
            def _():
                copy_c32(u - 1).wait()

    def chip_sum_last():
        @pl.when(outer)
        def _():
            copy_c16(UNITS - 1).wait()

        @pl.when(inner)
        def _():
            copy_c32(UNITS - 1).wait()

    def valid(u):
        return jnp.logical_and(u >= 0, u < UNITS)

    def tick(s):
        @pl.when(outer)
        def _():
            v = s - 3 * HOP

            @pl.when(valid(v))
            def _():
                @pl.when(v >= 4)
                def _():
                    copy_p_outer(v - 4).wait_send()

                copy_f(v).wait_recv()
                copy_p_outer(v).start()

            @pl.when(valid(s))
            def _():
                @pl.when(s >= RING)
                def _():
                    copy_a(s - RING).wait_send()

                copy_a(s).start()

        @pl.when(inner)
        def _():
            w = s - HOP

            @pl.when(valid(w + 1))
            def _():
                load_c32(w + 1).start()

            v = s - 2 * HOP

            @pl.when(valid(v))
            def _():
                @pl.when(v >= 4)
                def _():
                    copy_f(v - 4).wait_send()
                    copy_p_inner(v - 4).wait_send()
                    copy_l(v - 4).wait()

                copy_b(v).wait_recv()
                r = lax.rem(v, RING)
                fbuf[lax.rem(v, 4)] = (dbuf[r].astype(F32) + bbuf[r].astype(F32)).astype(BF)
                copy_f(v).start()
                copy_p_inner(v).start()
                copy_l(v).start()
                copy_b(v).wait_send()

            @pl.when(valid(w))
            def _():
                r = lax.rem(w, RING)
                load_c32(w).wait()
                copy_a(w).wait_recv()
                dbuf[r] = (cfb[lax.rem(w, 2)] + abuf[r].astype(F32)).astype(BF)
                copy_b(w).start()

    zero = jnp.int32(0)
    load_dy(zero).start()
    start(load_hidden(zero))
    start(load_weights(zero))

    @pl.loop(0, BLOCKS)
    def _(b):
        load_dy(b).wait()
        rows = ds(b, rb)

        @pl.loop(0, JT)
        def _(j):
            g = b * JT + j
            s = lax.rem(g, 2)
            wait(load_hidden(g))

            @pl.when(g + 1 < BLOCKS * JT)
            def _():
                start(load_hidden(g + 1))

            dh = dot(dyb[...], wdb[s], 1, 1)
            gv, uv = gb[s].astype(F32), ub[s].astype(F32)
            sig = jax.nn.sigmoid(gv)
            silu = gv * sig
            cols = ds(j, jb)
            hid_all[rows, cols] = (silu * uv).astype(BF)
            du_all[rows, cols] = (dh * silu).astype(BF)
            dg_all[rows, cols] = (dh * uv * (sig + silu * (1.0 - sig))).astype(BF)

            @pl.when(jnp.logical_and(b >= 1, jnp.logical_or(j == 2, j == 5)))
            def _():
                tick(6 * b - 2 + (j >= 5).astype(jnp.int32))

        @pl.when(b + 1 < BLOCKS)
        def _():
            load_dy(b + 1).start()

        @pl.when(b + 1 == BLOCKS)
        def _():
            load_x(zero, zero).start()

        @pl.loop(0, NT)
        def _(n):
            u = b * NT + n
            s = lax.rem(u, 2)

            @pl.when(u >= 1)
            def _():
                chip_sum(u - 1)

            wait(load_weights(u))

            @pl.when(u + 1 < UNITS)
            def _():
                start(load_weights(u + 1))

            @pl.when(u >= 4)
            def _():
                copy_x(u - 4).wait_send()

            term = dot(dg_all[rows, :], wgb[s], 1, 1) + dot(du_all[rows, :], wub[s], 1, 1)
            o = lax.rem(u, 4)
            first, second = term[:hb], term[hb:]
            own[o] = jnp.where(c == 0, first, second)
            tsend[o] = jnp.where(c == 0, second, first).astype(BF)
            copy_x(u).start()

            here = functools.reduce(jnp.logical_or, [n == k for k in (2, 4, 7, 9)])

            @pl.when(here)
            def _():
                tick(6 * b + sum((n >= k).astype(jnp.int32) for k in (4, 7, 9)))

    last = jnp.int32(UNITS - 1)
    chip_sum(last)
    chip_sum_last()
    for k in range(UNITS - 4, UNITS):
        copy_x(jnp.int32(k)).wait_send()

    base = 6 * BLOCKS - 2

    def out_g(i):
        s = lax.rem(i, 2)
        return (
            local(og.at[s], dwg.at[ds(i, ib), :], s_og.at[s]),
            local(ou.at[s], dwu.at[ds(i, ib), :], s_ou.at[s]),
        )

    steps_x = 2 * XT

    @pl.loop(0, steps_x)
    def _(i):
        m, h = i // 2, lax.rem(i, 2)
        s = lax.rem(m, 2)

        @pl.when(h == 0)
        def _():
            load_x(m, s).wait()

            @pl.when(m + 1 < XT)
            def _():
                load_x(m + 1, 1 - s).start()

            @pl.when(m + 1 == XT)
            def _():
                load_dyt(zero, 1 - s).start()

        @pl.when(i >= 2)
        def _():
            wait(out_g(i - 2))

        xt = xd[s, :, ds(h, ib)]
        e = lax.rem(i, 2)
        og[e] = dot(xt, dg_all[...], 0, 0).astype(BF)
        ou[e] = dot(xt, du_all[...], 0, 0).astype(BF)
        start(out_g(i))

        @pl.when(lax.rem(i, 4) < 3)
        def _():
            tick(base + (i // 4) * 3 + lax.rem(i, 4))

    wait(out_g(jnp.int32(steps_x - 2)))
    wait(out_g(jnp.int32(steps_x - 1)))

    base2 = base + (steps_x // 4) * 3

    def out_d(k):
        s = lax.rem(k, 2)
        p, q = k // JT, lax.rem(k, JT)
        return local(od.at[s], dwd.at[ds(q, jb), ds(p, xb)], s_od.at[s])

    steps_d = XT * JT

    @pl.loop(0, steps_d)
    def _(k):
        p, q = k // JT, lax.rem(k, JT)
        s = lax.rem(p + XT, 2)

        @pl.when(q == 0)
        def _():
            load_dyt(p, s).wait()

            @pl.when(p + 1 < XT)
            def _():
                load_dyt(p + 1, 1 - s).start()

        @pl.when(k >= 2)
        def _():
            out_d(k - 2).wait()

        od[lax.rem(k, 2)] = dot(hid_all[:, ds(q, jb)], xd[s], 0, 0).astype(BF)
        out_d(k).start()

        @pl.when(lax.rem(k, 9) == 4)
        def _():
            tick(base2 + k // 9)

    out_d(jnp.int32(steps_d - 2)).wait()
    out_d(jnp.int32(steps_d - 1)).wait()

    done = base2 + steps_d // 9 + 1

    @pl.loop(done, UNITS + 3 * HOP)
    def _(s):
        tick(s)

    @pl.when(outer)
    def _():
        @pl.loop(UNITS - RING, UNITS)
        def _(u):
            copy_a(u).wait_send()

        @pl.loop(UNITS - 4, UNITS)
        def _(u):
            copy_p_outer(u).wait_send()

    @pl.when(inner)
    def _():
        @pl.loop(UNITS - 4, UNITS)
        def _(u):
            copy_f(u).wait_send()
            copy_p_inner(u).wait_send()
            copy_l(u).wait()

    @pl.loop(0, UNITS)
    def _(u):
        remote(part(u, 1 - c), part(u, 1 - c), p_send.at[0], p_recv.at[u], partner).wait_recv()


def solution(mesh):
    def step(x, dy, gate, up, w_gate, w_up, w_down):
        rows, d = x.shape
        f = gate.shape[1]
        rb, cb, jb, xb = rows // BLOCKS, d // NT, f // JT, d // XT
        hb, ib = rb // 2, xb // 2
        like = [jax.ShapeDtypeStruct(a.shape, a.dtype) for a in (x, w_gate, w_up, w_down)]
        like += [jax.ShapeDtypeStruct((UNITS, hb, cb), BF), jax.ShapeDtypeStruct((UNITS, hb, cb), F32)]
        dma = pltpu.SemaphoreType.DMA
        vm = pltpu.VMEM
        scratch = [
            vm((rows, f), BF), vm((rows, f), BF), vm((rows, f), BF),
            vm((rb, d), BF), vm((2, jb, d), BF), vm((2, rb, jb), BF), vm((2, rb, jb), BF),
            vm((2, cb, f), BF), vm((2, cb, f), BF), vm((2, rows, xb), BF),
            vm((2, ib, f), BF), vm((2, ib, f), BF), vm((2, jb, xb), BF),
            vm((4, hb, cb), BF), vm((4, hb, cb), BF), vm((4, hb, cb), F32), vm((2, hb, cb), BF),
            vm((RING, hb, cb), BF), vm((RING, hb, cb), BF), vm((RING, hb, cb), BF), vm((4, hb, cb), BF), vm((2, hb, cb), F32),
            dma(()), dma((2,)), dma((2,)), dma((2,)), dma((2,)), dma((2,)), dma((2,)), dma((2,)), dma((2,)), dma((2,)),
            dma((4,)), dma((4,)), dma((2,)), dma((2,)), dma((RING,)), dma((RING,)), dma((RING,)), dma((RING,)),
            dma((4,)), dma((UNITS,)), dma((4,)), dma((UNITS,)), dma((4,)),
        ]
        outs = pl.pallas_call(
            kernel,
            out_shape=like,
            in_specs=[pl.BlockSpec(memory_space=pl.ANY)] * 7,
            out_specs=[pl.BlockSpec(memory_space=pl.ANY)] * 6,
            scratch_shapes=scratch,
            compiler_params=pltpu.CompilerParams(
                collective_id=0, has_side_effects=True, vmem_limit_bytes=67_000_000
            ),
            name="mlp_backward",
        )(x, dy, gate, up, w_gate, w_up, w_down)
        return tuple(outs[:4])

    tokens, columns, rows = P("dp", None), P(None, "tp"), P("tp", None)
    return jax.shard_map(
        step,
        mesh=mesh,
        in_specs=(tokens, tokens, P("dp", "tp"), P("dp", "tp"), columns, columns, rows),
        out_specs=(tokens, P("dp", "tp"), P("dp", "tp"), P(("dp", "tp"), None)),
        check_vma=False,
    )
```

time: 625 us -> 392 us (0.63)
  Pallas kernels: 0 us -> 337 us
  matrix products: 328 us -> 0 us
  waiting for transfers between devices: 213 us -> 0 us
  between operations: 14.6 us -> 0.74 us
  local copies, waits for them, and re-layouts: 63.6 us -> 53.4 us
    pallas_call x0 -> x1, Pallas kernels: none -> 337 us  [step(): pl.pallas_call(kernel, out_shape=like, in_specs=[pl.BlockSpec(memory_spac...]
    dot_general x6 -> x0, matrix products: 328 us -> none  [the longest x1 66.8 us: step(): jnp.dot(d_up, w_up.T, preferred_element_type=jnp.float32)]
    psum x1 -> x0, waiting for transfers between devices: 213 us -> none  [step(): dx = lax.psum(term.astype(jnp.bfloat16), 'tp')]
    unnamed x9 -> x24, local copies, waits for them, and re-layouts: 63.6 us -> 53.4 us
  transfers between devices with their start and end apart: 1 -> 0, of which waited for: 1 -> 0; matrix products, arithmetic and copies ran while one was open for 33% -> 0% of each run, Pallas kernels for 0% -> 0%
where the time goes in v1:
time: 392 us; the launch traced here: 391 us
  Pallas kernels  337 us (86%)
  local copies, waits for them, and re-layouts  53.4 us (14%)
    pallas_call x1, Pallas kernels, step(): pl.pallas_call(kernel, out_shape=like, in_specs=[pl.BlockSpec(memory_spac...  337 us
    unnamed x24, local copies, waits for them, and re-layouts  53.4 us

profile of v1, /device:TPU:0, one launch (start us, length us, event | category | flops | bytes accessed | tf_op | source)
XLA Modules:
  0.0 391.5 jit_solution(14053027550375272718)
XLA Ops:
  0.6 337.3 %mlp_backward.1 = (bf16[2048,5120]{1,0:T(8,128)(2,1)}, bf16[5120,1792]{1,0:T(8,128)(2,1)}, bf16[5120,1792]{1,0:T(8,128)(2,1)}, bf16[1792,5120]{1,0:T(8,128)(2,1)...) custom-call(bf16[2048,5120]{1,0:T(8,128)(2,1)} %x.1, bf16[2048,5120]{1,0:T(8,128)(2,1)} %dy.1, ...), custom_call_target="tpu_custom_call" | custom-call | tf_op jit(solution)/shard_map/mlp_backward/pallas_call | solution.py:438
  338.0 0.0 slice-start.5
  338.0 0.0 slice-start.6
  338.0 0.0 slice-start.7
  338.0 19.4 %copy.15 = bf16[2048,5120]{1,0:T(8,128)(2,1)} copy(bf16[2048,5120]{1,0:T(8,128)(2,1)} %get-tuple-element.16) | data formatting | bytes 41943040
  357.4 0.0 slice-start.8
  357.4 0.0 slice-start.9
  357.4 0.0 slice-start
  357.4 0.0 slice-start.2
  357.4 19.2 %copy.16 = bf16[5120,1792]{1,0:T(8,128)(2,1)} copy(bf16[5120,1792]{1,0:T(8,128)(2,1)} %get-tuple-element.17) | data formatting | bytes 36700160
  376.6 0.0 slice-done.5
  376.6 0.0 slice-done.6
  376.6 0.0 slice-done.7
  376.6 0.0 slice-done.8
  376.6 0.0 slice-done.9
  376.6 0.0 slice-start.3
  376.6 0.0 slice-start.4
  376.7 8.1 %copy.17 = bf16[5120,1792]{1,0:T(8,128)(2,1)} copy(bf16[5120,1792]{1,0:T(8,128)(2,1)S(1)} %bitcast.3) | data formatting | bytes 36700160
  384.8 0.0 slice-done
  384.8 0.0 slice-done.1
  384.8 0.0 slice-done.2
  384.8 0.0 slice-done.3
  384.8 0.0 slice-done.4
  384.8 6.7 %copy.18 = bf16[1792,5120]{1,0:T(8,128)(2,1)} copy(bf16[1792,5120]{1,0:T(8,128)(2,1)S(1)} %bitcast.1) | data formatting | bytes 36700160
  (3 shorter events, 0.0 us)
Async XLA Ops:
  338.0 38.6 %slice-start.5 = ((s8[18350080]{0:T(1024)(128)(4,1)}), s8[4194304]{0:T(1024)(128)(4,1)S(1)}, s32[]{:S(2)}) async-start(s8[18350080]{0:T(1024)(128)(4,1)} %bitcast.2), calls=%async_computation.5 | async-start | bytes 8388608
  338.0 38.6 %slice-start.6 = ((s8[18350080]{0:T(1024)(128)(4,1)}), s8[4194304]{0:T(1024)(128)(4,1)S(1)}, s32[]{:S(2)}) async-start(s8[18350080]{0:T(1024)(128)(4,1)} %bitcast.2), calls=%async_computation.6 | async-start | bytes 8388608
  338.0 38.6 %slice-start.7 = ((s8[18350080]{0:T(1024)(128)(4,1)}), s8[4194304]{0:T(1024)(128)(4,1)S(1)}, s32[]{:S(2)}) async-start(s8[18350080]{0:T(1024)(128)(4,1)} %bitcast.2), calls=%async_computation.7 | async-start | bytes 8388608
  357.4 19.2 %slice-start.8 = ((s8[18350080]{0:T(1024)(128)(4,1)}), s8[4194304]{0:T(1024)(128)(4,1)S(1)}, s32[]{:S(2)}) async-start(s8[18350080]{0:T(1024)(128)(4,1)} %bitcast.2), calls=%async_computation.8 | async-start | bytes 8388608
  357.4 19.2 %slice-start.9 = ((s8[18350080]{0:T(1024)(128)(4,1)}), s8[1572864]{0:T(1024)(128)(4,1)S(1)}, s32[]{:S(2)}) async-start(s8[18350080]{0:T(1024)(128)(4,1)} %bitcast.2), calls=%async_computation.9 | async-start | bytes 3145728
  357.4 27.4 %slice-start = ((s8[18350080]{0:T(1024)(128)(4,1)}), s8[4194304]{0:T(1024)(128)(4,1)S(1)}, s32[]{:S(2)}) async-start(s8[18350080]{0:T(1024)(128)(4,1)} %bitcast), calls=%async_computation | async-start | bytes 8388608
  357.4 27.4 %slice-start.1 = ((s8[18350080]{0:T(1024)(128)(4,1)}), s8[4194304]{0:T(1024)(128)(4,1)S(1)}, s32[]{:S(2)}) async-start(s8[18350080]{0:T(1024)(128)(4,1)} %bitcast), calls=%async_computation.1 | async-start | bytes 8388608
  357.4 27.4 %slice-start.2 = ((s8[18350080]{0:T(1024)(128)(4,1)}), s8[4194304]{0:T(1024)(128)(4,1)S(1)}, s32[]{:S(2)}) async-start(s8[18350080]{0:T(1024)(128)(4,1)} %bitcast), calls=%async_computation.2 | async-start | bytes 8388608
  376.6 8.1 %slice-start.3 = ((s8[18350080]{0:T(1024)(128)(4,1)}), s8[4194304]{0:T(1024)(128)(4,1)S(1)}, s32[]{:S(2)}) async-start(s8[18350080]{0:T(1024)(128)(4,1)} %bitcast), calls=%async_computation.3 | async-start | bytes 8388608
  376.6 8.1 %slice-start.4 = ((s8[18350080]{0:T(1024)(128)(4,1)}), s8[1572864]{0:T(1024)(128)(4,1)S(1)}, s32[]{:S(2)}) async-start(s8[18350080]{0:T(1024)(128)(4,1)} %bitcast), calls=%async_computation.4 | async-start | bytes 3145728

commit v2 on v1

--- a/solution.py
+++ b/solution.py
@@ -11,7 +11,10 @@
 MESH = pl.DeviceIdType.MESH
 BLOCKS, JT, NT, XT = 4, 7, 10, 10
 UNITS = BLOCKS * NT
-RING, HOP = 8, 2
+RING = 8
+HALVES = 2 * (UNITS + 6)
+CHUNKS, DT = 32, 5
+AT_FIRST, AT_HIDDEN, AT_DX = (2, 3, 4, 5, 6, 7, 8, 9), (0, 1, 3, 4, 6), (0, 1, 2, 3, 4, 5, 6, 7, 8, 9)
 
 
 def dot(a, b, ca, cb):
@@ -20,10 +23,10 @@
 
 def kernel(
     x, dy, gate, up, wg, wu, wd,
-    dx, dwg, dwu, dwd, chip16, chip32,
-    dg_all, du_all, hid_all, dyb, wdb, gb, ub, wgb, wub, xd, og, ou, od,
+    dx, dwg, dwu, hid, chip16, chip32,
+    dg_all, du_all, hs, dyb, wdb, gb, ub, wgb, wub, xd, og, ou,
     tsend, xrecv, own, cst, abuf, bbuf, dbuf, fbuf, cfb,
-    s_dy, s_wd, s_g, s_u, s_wg, s_wu, s_xd, s_og, s_ou, s_od,
+    s_dy, s_wd, s_g, s_u, s_wg, s_wu, s_xd, s_og, s_ou, s_h,
     x_send, x_recv, s_c, s_cf, a_send, a_recv, b_send, b_recv, f_send, f_recv, p_send, p_recv, s_l,
 ):
     rb, cb = dyb.shape[0], wgb.shape[1]
@@ -84,9 +87,6 @@
     def load_x(m, s):
         return local(x.at[:, ds(m, xb)], xd.at[s], s_xd.at[s])
 
-    def load_dyt(m, s):
-        return local(dy.at[:, ds(m, xb)], xd.at[s], s_xd.at[s])
-
     def start(copies):
         for copy in copies:
             copy.start()
@@ -169,63 +169,80 @@
     def valid(u):
         return jnp.logical_and(u >= 0, u < UNITS)
 
-    def tick(s):
-        @pl.when(outer)
-        def _():
-            v = s - 3 * HOP
-
-            @pl.when(valid(v))
-            def _():
-                @pl.when(v >= 4)
-                def _():
-                    copy_p_outer(v - 4).wait_send()
-
-                copy_f(v).wait_recv()
-                copy_p_outer(v).start()
-
-            @pl.when(valid(s))
-            def _():
-                @pl.when(s >= RING)
-                def _():
-                    copy_a(s - RING).wait_send()
-
-                copy_a(s).start()
-
-        @pl.when(inner)
-        def _():
-            w = s - HOP
-
-            @pl.when(valid(w + 1))
-            def _():
-                load_c32(w + 1).start()
-
-            v = s - 2 * HOP
-
-            @pl.when(valid(v))
-            def _():
-                @pl.when(v >= 4)
-                def _():
-                    copy_f(v - 4).wait_send()
-                    copy_p_inner(v - 4).wait_send()
-                    copy_l(v - 4).wait()
-
-                copy_b(v).wait_recv()
-                r = lax.rem(v, RING)
-                fbuf[lax.rem(v, 4)] = (dbuf[r].astype(F32) + bbuf[r].astype(F32)).astype(BF)
-                copy_f(v).start()
-                copy_p_inner(v).start()
-                copy_l(v).start()
-                copy_b(v).wait_send()
-
-            @pl.when(valid(w))
-            def _():
-                r = lax.rem(w, RING)
-                load_c32(w).wait()
-                copy_a(w).wait_recv()
-                dbuf[r] = (cfb[lax.rem(w, 2)] + abuf[r].astype(F32)).astype(BF)
-                copy_b(w).start()
+    def first_half(s):
+        @pl.when(jnp.logical_and(outer, valid(s)))
+        def _():
+            @pl.when(s >= RING)
+            def _():
+                copy_a(s - RING).wait_send()
+
+            copy_a(s).start()
+
+        w = s - 2
+
+        @pl.when(jnp.logical_and(inner, valid(w)))
+        def _():
+            r = lax.rem(w, RING)
+            load_c32(w).wait()
+            copy_a(w).wait_recv()
+            dbuf[r] = (cfb[lax.rem(w, 2)] + abuf[r].astype(F32)).astype(BF)
+            copy_b(w).start()
+
+    def second_half(s):
+        @pl.when(jnp.logical_and(inner, valid(s - 1)))
+        def _():
+            load_c32(s - 1).start()
+
+        v = s - 4
+
+        @pl.when(jnp.logical_and(inner, valid(v)))
+        def _():
+            @pl.when(v >= 4)
+            def _():
+                copy_f(v - 4).wait_send()
+                copy_p_inner(v - 4).wait_send()
+                copy_l(v - 4).wait()
+
+            copy_b(v).wait_recv()
+            r = lax.rem(v, RING)
+            fbuf[lax.rem(v, 4)] = (dbuf[r].astype(F32) + bbuf[r].astype(F32)).astype(BF)
+            copy_f(v).start()
+            copy_p_inner(v).start()
+            copy_l(v).start()
+            copy_b(v).wait_send()
+
+        q = s - 6
+
+        @pl.when(jnp.logical_and(outer, valid(q)))
+        def _():
+            @pl.when(q >= 4)
+            def _():
+                copy_p_outer(q - 4).wait_send()
+
+            copy_f(q).wait_recv()
+            copy_p_outer(q).start()
+
+    def half_step(h):
+        @pl.when(lax.rem(h, 2) == 0)
+        def _():
+            first_half(h // 2)
+
+        @pl.when(lax.rem(h, 2) == 1)
+        def _():
+            second_half(h // 2)
+
+    def count(i, steps):
+        return sum((i > k).astype(jnp.int32) for k in steps)
+
+    def among(i, steps):
+        return functools.reduce(jnp.logical_or, [i == k for k in steps])
+
+    def out_h(g):
+        b, j, s = g // JT, lax.rem(g, JT), lax.rem(g, 2)
+        return local(hs.at[s], hid.at[ds(b, rb), ds(j, jb)], s_h.at[s])
 
     zero = jnp.int32(0)
+    per_block = len(AT_HIDDEN) + len(AT_DX)
     load_dy(zero).start()
     start(load_hidden(zero))
     start(load_weights(zero))
@@ -250,13 +267,20 @@
             sig = jax.nn.sigmoid(gv)
             silu = gv * sig
             cols = ds(j, jb)
-            hid_all[rows, cols] = (silu * uv).astype(BF)
+
+            @pl.when(g >= 2)
+            def _():
+                out_h(g - 2).wait()
+
+            hs[s] = (silu * uv).astype(BF)
             du_all[rows, cols] = (dh * silu).astype(BF)
             dg_all[rows, cols] = (dh * uv * (sig + silu * (1.0 - sig))).astype(BF)
 
-            @pl.when(jnp.logical_and(b >= 1, jnp.logical_or(j == 2, j == 5)))
-            def _():
-                tick(6 * b - 2 + (j >= 5).astype(jnp.int32))
+            out_h(g).start()
+
+            @pl.when(jnp.logical_and(b >= 1, among(j, AT_HIDDEN)))
+            def _():
+                half_step(len(AT_FIRST) + per_block * (b - 1) + count(j, AT_HIDDEN))
 
         @pl.when(b + 1 < BLOCKS)
         def _():
@@ -270,10 +294,6 @@
         def _(n):
             u = b * NT + n
             s = lax.rem(u, 2)
-
-            @pl.when(u >= 1)
-            def _():
-                chip_sum(u - 1)
 
             wait(load_weights(u))
 
@@ -292,11 +312,17 @@
             tsend[o] = jnp.where(c == 0, second, first).astype(BF)
             copy_x(u).start()
 
-            here = functools.reduce(jnp.logical_or, [n == k for k in (2, 4, 7, 9)])
-
-            @pl.when(here)
-            def _():
-                tick(6 * b + sum((n >= k).astype(jnp.int32) for k in (4, 7, 9)))
+            @pl.when(u >= 1)
+            def _():
+                chip_sum(u - 1)
+
+            @pl.when(jnp.logical_and(b == 0, among(n, AT_FIRST)))
+            def _():
+                half_step(count(n, AT_FIRST))
+
+            @pl.when(jnp.logical_and(b >= 1, among(n, AT_DX)))
+            def _():
+                half_step(len(AT_FIRST) + per_block * (b - 1) + len(AT_HIDDEN) + count(n, AT_DX))
 
     last = jnp.int32(UNITS - 1)
     chip_sum(last)
@@ -304,7 +330,9 @@
     for k in range(UNITS - 4, UNITS):
         copy_x(jnp.int32(k)).wait_send()
 
-    base = 6 * BLOCKS - 2
+    out_h(jnp.int32(BLOCKS * JT - 2)).wait()
+    out_h(jnp.int32(BLOCKS * JT - 1)).wait()
+    base = len(AT_FIRST) + per_block * (BLOCKS - 1)
 
     def out_g(i):
         s = lax.rem(i, 2)
@@ -328,10 +356,6 @@
             def _():
                 load_x(m + 1, 1 - s).start()
 
-            @pl.when(m + 1 == XT)
-            def _():
-                load_dyt(zero, 1 - s).start()
-
         @pl.when(i >= 2)
         def _():
             wait(out_g(i - 2))
@@ -339,57 +363,17 @@
         xt = xd[s, :, ds(h, ib)]
         e = lax.rem(i, 2)
         og[e] = dot(xt, dg_all[...], 0, 0).astype(BF)
+        half_step(base + 2 * i)
         ou[e] = dot(xt, du_all[...], 0, 0).astype(BF)
         start(out_g(i))
-
-        @pl.when(lax.rem(i, 4) < 3)
-        def _():
-            tick(base + (i // 4) * 3 + lax.rem(i, 4))
+        half_step(base + 2 * i + 1)
 
     wait(out_g(jnp.int32(steps_x - 2)))
     wait(out_g(jnp.int32(steps_x - 1)))
 
-    base2 = base + (steps_x // 4) * 3
-
-    def out_d(k):
-        s = lax.rem(k, 2)
-        p, q = k // JT, lax.rem(k, JT)
-        return local(od.at[s], dwd.at[ds(q, jb), ds(p, xb)], s_od.at[s])
-
-    steps_d = XT * JT
-
-    @pl.loop(0, steps_d)
-    def _(k):
-        p, q = k // JT, lax.rem(k, JT)
-        s = lax.rem(p + XT, 2)
-
-        @pl.when(q == 0)
-        def _():
-            load_dyt(p, s).wait()
-
-            @pl.when(p + 1 < XT)
-            def _():
-                load_dyt(p + 1, 1 - s).start()
-
-        @pl.when(k >= 2)
-        def _():
-            out_d(k - 2).wait()
-
-        od[lax.rem(k, 2)] = dot(hid_all[:, ds(q, jb)], xd[s], 0, 0).astype(BF)
-        out_d(k).start()
-
-        @pl.when(lax.rem(k, 9) == 4)
-        def _():
-            tick(base2 + k // 9)
-
-    out_d(jnp.int32(steps_d - 2)).wait()
-    out_d(jnp.int32(steps_d - 1)).wait()
-
-    done = base2 + steps_d // 9 + 1
-
-    @pl.loop(done, UNITS + 3 * HOP)
-    def _(s):
-        tick(s)
+    @pl.loop(base + 2 * steps_x, HALVES)
+    def _(h):
+        half_step(h)
 
     @pl.when(outer)
     def _():
@@ -414,6 +398,88 @@
         remote(part(u, 1 - c), part(u, 1 - c), p_send.at[0], p_recv.at[u], partner).wait_recv()
 
 
+def down_kernel(
+    hid, dy, dx, dwg, dwu, dx_out, dwg_out, dwu_out, dwd, hv, xd, od, r0, r1, r2, s_h, s_xd, s_od, s_in, s_out
+):
+    jb, xb = hv.shape[2], xd.shape[2]
+    moves = ((dx, dx_out, r0), (dwg, dwg_out, r1), (dwu, dwu_out, r2))
+    steps = DT * JT
+
+    def local(src, dst, sem):
+        return pltpu.make_async_copy(src, dst, sem)
+
+    def ds(i, n):
+        return pl.ds(pl.multiple_of(i * n, n), n)
+
+    def load_h(q):
+        return local(hid.at[:, ds(q, jb)], hv.at[q], s_h.at[q])
+
+    def load_dy(p):
+        return local(dy.at[:, ds(p, xb)], xd.at[lax.rem(p, 2)], s_xd.at[lax.rem(p, 2)])
+
+    def read(a, k):
+        src, _, ring = moves[a]
+        return local(src.at[ds(k, ring.shape[1]), :], ring.at[lax.rem(k, RING)], s_in.at[a, lax.rem(k, RING)])
+
+    def write(a, k):
+        _, dst, ring = moves[a]
+        return local(ring.at[lax.rem(k, RING)], dst.at[ds(k, ring.shape[1]), :], s_out.at[a, lax.rem(k, RING)])
+
+    def out_d(k):
+        p, q, s = k // JT, lax.rem(k, JT), lax.rem(k, 2)
+        return local(od.at[s], dwd.at[ds(q, jb), ds(p, xb)], s_od.at[s])
+
+    load_dy(jnp.int32(0)).start()
+    for q in range(JT):
+        load_h(jnp.int32(q)).start()
+        if q < 4:
+            for a in range(3):
+                read(a, jnp.int32(q)).start()
+
+    @pl.loop(0, steps)
+    def _(k):
+        p, q = k // JT, lax.rem(k, JT)
+
+        @pl.when(k < CHUNKS)
+        def _():
+            for a in range(3):
+                read(a, k).wait()
+                write(a, k).start()
+
+                @pl.when(k >= 4)
+                def _():
+                    write(a, k - 4).wait()
+
+                @pl.when(k + 4 < CHUNKS)
+                def _():
+                    read(a, k + 4).start()
+
+        @pl.when(q == 0)
+        def _():
+            load_dy(p).wait()
+
+            @pl.when(p + 1 < DT)
+            def _():
+                load_dy(p + 1).start()
+
+        @pl.when(p == 0)
+        def _():
+            load_h(q).wait()
+
+        @pl.when(k >= 2)
+        def _():
+            out_d(k - 2).wait()
+
+        od[lax.rem(k, 2)] = dot(hv[q], xd[lax.rem(p, 2)], 0, 0).astype(BF)
+        out_d(k).start()
+
+    for k in (2, 1):
+        out_d(jnp.int32(steps - k)).wait()
+    for k in (4, 3, 2, 1):
+        for a in range(3):
+            write(a, jnp.int32(CHUNKS - k)).wait()
+
+
 def solution(mesh):
     def step(x, dy, gate, up, w_gate, w_up, w_down):
         rows, d = x.shape
@@ -421,32 +487,47 @@
         rb, cb, jb, xb = rows // BLOCKS, d // NT, f // JT, d // XT
         hb, ib = rb // 2, xb // 2
         like = [jax.ShapeDtypeStruct(a.shape, a.dtype) for a in (x, w_gate, w_up, w_down)]
-        like += [jax.ShapeDtypeStruct((UNITS, hb, cb), BF), jax.ShapeDtypeStruct((UNITS, hb, cb), F32)]
-        dma = pltpu.SemaphoreType.DMA
-        vm = pltpu.VMEM
+        between = [jax.ShapeDtypeStruct((rows, f), BF)]
+        between += [jax.ShapeDtypeStruct((UNITS, hb, cb), BF), jax.ShapeDtypeStruct((UNITS, hb, cb), F32)]
+        dma, vm = pltpu.SemaphoreType.DMA, pltpu.VMEM
+        hbm = pl.BlockSpec(memory_space=pl.ANY)
         scratch = [
-            vm((rows, f), BF), vm((rows, f), BF), vm((rows, f), BF),
+            vm((rows, f), BF), vm((rows, f), BF), vm((2, rb, jb), BF),
             vm((rb, d), BF), vm((2, jb, d), BF), vm((2, rb, jb), BF), vm((2, rb, jb), BF),
             vm((2, cb, f), BF), vm((2, cb, f), BF), vm((2, rows, xb), BF),
-            vm((2, ib, f), BF), vm((2, ib, f), BF), vm((2, jb, xb), BF),
+            vm((2, ib, f), BF), vm((2, ib, f), BF),
             vm((4, hb, cb), BF), vm((4, hb, cb), BF), vm((4, hb, cb), F32), vm((2, hb, cb), BF),
             vm((RING, hb, cb), BF), vm((RING, hb, cb), BF), vm((RING, hb, cb), BF), vm((4, hb, cb), BF), vm((2, hb, cb), F32),
             dma(()), dma((2,)), dma((2,)), dma((2,)), dma((2,)), dma((2,)), dma((2,)), dma((2,)), dma((2,)), dma((2,)),
             dma((4,)), dma((4,)), dma((2,)), dma((2,)), dma((RING,)), dma((RING,)), dma((RING,)), dma((RING,)),
             dma((4,)), dma((UNITS,)), dma((4,)), dma((UNITS,)), dma((4,)),
         ]
-        outs = pl.pallas_call(
+        dx, dwg, dwu, hid, *_ = pl.pallas_call(
             kernel,
-            out_shape=like,
-            in_specs=[pl.BlockSpec(memory_space=pl.ANY)] * 7,
-            out_specs=[pl.BlockSpec(memory_space=pl.ANY)] * 6,
+            out_shape=like[:3] + between,
+            in_specs=[hbm] * 7,
+            out_specs=[hbm] * 6,
             scratch_shapes=scratch,
             compiler_params=pltpu.CompilerParams(
                 collective_id=0, has_side_effects=True, vmem_limit_bytes=67_000_000
             ),
             name="mlp_backward",
         )(x, dy, gate, up, w_gate, w_up, w_down)
-        return tuple(outs[:4])
+        return tuple(
+            pl.pallas_call(
+                down_kernel,
+                out_shape=like,
+                in_specs=[hbm] * 5,
+                out_specs=[hbm] * 4,
+                scratch_shapes=[
+                    vm((JT, rows, jb), BF), vm((2, rows, d // DT), BF), vm((2, jb, d // DT), BF),
+                    vm((RING, rows // CHUNKS, d), BF), vm((RING, d // CHUNKS, f), BF), vm((RING, d // CHUNKS, f), BF),
+                    dma((JT,)), dma((2,)), dma((2,)), dma((3, RING)), dma((3, RING)),
+                ],
+                compiler_params=pltpu.CompilerParams(vmem_limit_bytes=67_000_000),
+                name="mlp_down",
+            )(hid, dy, dx, dwg, dwu)
+        )
 
     tokens, columns, rows = P("dp", None), P(None, "tp"), P("tp", None)
     return jax.shard_map(

time: 392 us -> 340 us (0.87)
  local copies, waits for them, and re-layouts: 53.4 us -> 0 us
    unnamed x24 -> x0, local copies, waits for them, and re-layouts: 53.4 us -> none
    pallas_call x1 -> x2, Pallas kernels: 337 us -> 340 us  [the longest x1 282 us: step(): pl.pallas_call(kernel, out_shape=like[:3] + between, in_specs=[hbm] * 7,...]
where the time goes in v2:
time: 340 us
  Pallas kernels  340 us (100%)
    pallas_call x1, Pallas kernels, step(): pl.pallas_call(kernel, out_shape=like[:3] + between, in_specs=[hbm] * 7,...  282 us
    pallas_call x1, Pallas kernels, step(): pl.pallas_call(down_kernel, out_shape=like, in_specs=[hbm] * 5, out_specs...  57.2 us

profile of v2, /device:TPU:0, one launch (start us, length us, event | category | flops | bytes accessed | tf_op | source)
XLA Modules:
  0.0 340.3 jit_solution(8483382301357432343)
XLA Ops:
  0.6 282.5 %mlp_backward.1 = (bf16[2048,5120]{1,0:T(8,128)(2,1)}, bf16[5120,1792]{1,0:T(8,128)(2,1)}, bf16[5120,1792]{1,0:T(8,128)(2,1)}, bf16[2048,1792]{1,0:T(8,128)(2,1)...) custom-call(bf16[2048,5120]{1,0:T(8,128)(2,1)} %x.1, bf16[2048,5120]{1,0:T(8,128)(2,1)} %dy.3, ...), custom_call_target="tpu_custom_call" | custom-call | tf_op jit(solution)/shard_map/mlp_backward/pallas_call | solution.py:505
  283.1 57.2 %mlp_down.1 = (bf16[2048,5120]{1,0:T(8,128)(2,1)}, bf16[5120,1792]{1,0:T(8,128)(2,1)}, bf16[5120,1792]{1,0:T(8,128)(2,1)}, bf16[1792,5120]{1,0:T(8,128)(2,1)}) custom-call(bf16[2048,1792]{1,0:T(8,128)(2,1)} %get-tuple-element.8.hid, bf16[2048,5120]{1,0:T(8,128)(2,1)} %dy.3, bf16[2048,5120]{1,0:T(8,128)(2,1)} %get-tuple-element.9.dx, ...), custom_call_target="tpu_custom_call" | custom-call | tf_op jit(solution)/shard_map/mlp_down/pallas_call | solution.py:517

commit v3 on v2

--- a/solution.py
+++ b/solution.py
@@ -13,7 +13,8 @@
 UNITS = BLOCKS * NT
 RING = 8
 HALVES = 2 * (UNITS + 6)
-CHUNKS, DT = 32, 5
+CHUNKS, DT = 32, 8
+EARLY = 2
 AT_FIRST, AT_HIDDEN, AT_DX = (2, 3, 4, 5, 6, 7, 8, 9), (0, 1, 3, 4, 6), (0, 1, 2, 3, 4, 5, 6, 7, 8, 9)
 
 
@@ -23,10 +24,10 @@
 
 def kernel(
     x, dy, gate, up, wg, wu, wd,
-    dx, dwg, dwu, hid, chip16, chip32,
-    dg_all, du_all, hs, dyb, wdb, gb, ub, wgb, wub, xd, og, ou,
+    dx, dwg, dwu, dwd, hid, chip16, chip32,
+    dg_all, du_all, hid_early, od, hs, dyb, wdb, gb, ub, wgb, wub, xd, og, ou,
     tsend, xrecv, own, cst, abuf, bbuf, dbuf, fbuf, cfb,
-    s_dy, s_wd, s_g, s_u, s_wg, s_wu, s_xd, s_og, s_ou, s_h,
+    s_dy, s_wd, s_g, s_u, s_wg, s_wu, s_xd, s_og, s_ou, s_od, s_h,
     x_send, x_recv, s_c, s_cf, a_send, a_recv, b_send, b_recv, f_send, f_recv, p_send, p_recv, s_l,
 ):
     rb, cb = dyb.shape[0], wgb.shape[1]
@@ -87,6 +88,9 @@
     def load_x(m, s):
         return local(x.at[:, ds(m, xb)], xd.at[s], s_xd.at[s])
 
+    def load_dyt(m, s):
+        return local(dy.at[:, ds(m, xb)], xd.at[s], s_xd.at[s])
+
     def start(copies):
         for copy in copies:
             copy.start()
@@ -273,6 +277,11 @@
                 out_h(g - 2).wait()
 
             hs[s] = (silu * uv).astype(BF)
+
+            @pl.when(j < EARLY)
+            def _():
+                hid_early[rows, cols] = hs[s]
+
             du_all[rows, cols] = (dh * silu).astype(BF)
             dg_all[rows, cols] = (dh * uv * (sig + silu * (1.0 - sig))).astype(BF)
 
@@ -356,6 +365,10 @@
             def _():
                 load_x(m + 1, 1 - s).start()
 
+            @pl.when(m + 1 == XT)
+            def _():
+                load_dyt(zero, 1 - s).start()
+
         @pl.when(i >= 2)
         def _():
             wait(out_g(i - 2))
@@ -363,15 +376,53 @@
         xt = xd[s, :, ds(h, ib)]
         e = lax.rem(i, 2)
         og[e] = dot(xt, dg_all[...], 0, 0).astype(BF)
-        half_step(base + 2 * i)
+        half_step(base + 3 * (i // 2) + 2 * h)
         ou[e] = dot(xt, du_all[...], 0, 0).astype(BF)
         start(out_g(i))
-        half_step(base + 2 * i + 1)
+
+        @pl.when(h == 0)
+        def _():
+            half_step(base + 3 * (i // 2) + 1)
 
     wait(out_g(jnp.int32(steps_x - 2)))
     wait(out_g(jnp.int32(steps_x - 1)))
 
-    @pl.loop(base + 2 * steps_x, HALVES)
+    base2 = base + 3 * XT
+
+    def out_d(k):
+        p, q, s = k // EARLY, lax.rem(k, EARLY), lax.rem(k, 2)
+        return local(od.at[s], dwd.at[ds(q, jb), ds(p, xb)], s_od.at[s])
+
+    steps_d = XT * EARLY
+
+    @pl.loop(0, steps_d)
+    def _(k):
+        p, q = k // EARLY, lax.rem(k, EARLY)
+        s = lax.rem(p + XT, 2)
+
+        @pl.when(q == 0)
+        def _():
+            load_dyt(p, s).wait()
+
+            @pl.when(p + 1 < XT)
+            def _():
+                load_dyt(p + 1, 1 - s).start()
+
+        @pl.when(k >= 2)
+        def _():
+            out_d(k - 2).wait()
+
+        od[lax.rem(k, 2)] = dot(hid_early[:, ds(q, jb)], xd[s], 0, 0).astype(BF)
+        out_d(k).start()
+
+        @pl.when(q == 0)
+        def _():
+            half_step(base2 + p)
+
+    out_d(jnp.int32(steps_d - 2)).wait()
+    out_d(jnp.int32(steps_d - 1)).wait()
+
+    @pl.loop(base2 + XT, HALVES)
     def _(h):
         half_step(h)
 
@@ -399,11 +450,12 @@
 
 
 def down_kernel(
-    hid, dy, dx, dwg, dwu, dx_out, dwg_out, dwu_out, dwd, hv, xd, od, r0, r1, r2, s_h, s_xd, s_od, s_in, s_out
+    hid, dy, dx, dwg, dwu, early, dx_out, dwg_out, dwu_out, dwd, hv, xd, od, r0, r1, r2, r3, s_h, s_xd, s_od, s_in, s_out
 ):
     jb, xb = hv.shape[2], xd.shape[2]
-    moves = ((dx, dx_out, r0), (dwg, dwg_out, r1), (dwu, dwu_out, r2))
-    steps = DT * JT
+    moves = ((dx, dx_out, r0), (dwg, dwg_out, r1), (dwu, dwu_out, r2), (early, dwd, r3))
+    late = JT - EARLY
+    steps = DT * late
 
     def local(src, dst, sem):
         return pltpu.make_async_copy(src, dst, sem)
@@ -412,7 +464,7 @@
         return pl.ds(pl.multiple_of(i * n, n), n)
 
     def load_h(q):
-        return local(hid.at[:, ds(q, jb)], hv.at[q], s_h.at[q])
+        return local(hid.at[:, ds(q + EARLY, jb)], hv.at[q], s_h.at[q])
 
     def load_dy(p):
         return local(dy.at[:, ds(p, xb)], xd.at[lax.rem(p, 2)], s_xd.at[lax.rem(p, 2)])
@@ -426,23 +478,23 @@
         return local(ring.at[lax.rem(k, RING)], dst.at[ds(k, ring.shape[1]), :], s_out.at[a, lax.rem(k, RING)])
 
     def out_d(k):
-        p, q, s = k // JT, lax.rem(k, JT), lax.rem(k, 2)
-        return local(od.at[s], dwd.at[ds(q, jb), ds(p, xb)], s_od.at[s])
+        p, q, s = k // late, lax.rem(k, late), lax.rem(k, 2)
+        return local(od.at[s], dwd.at[ds(q + EARLY, jb), ds(p, xb)], s_od.at[s])
 
     load_dy(jnp.int32(0)).start()
-    for q in range(JT):
+    for q in range(late):
         load_h(jnp.int32(q)).start()
         if q < 4:
-            for a in range(3):
+            for a in range(4):
                 read(a, jnp.int32(q)).start()
 
     @pl.loop(0, steps)
     def _(k):
-        p, q = k // JT, lax.rem(k, JT)
+        p, q = k // late, lax.rem(k, late)
 
         @pl.when(k < CHUNKS)
         def _():
-            for a in range(3):
+            for a in range(4):
                 read(a, k).wait()
                 write(a, k).start()
 
@@ -476,7 +528,7 @@
     for k in (2, 1):
         out_d(jnp.int32(steps - k)).wait()
     for k in (4, 3, 2, 1):
-        for a in range(3):
+        for a in range(4):
             write(a, jnp.int32(CHUNKS - k)).wait()
 
 
@@ -487,26 +539,26 @@
         rb, cb, jb, xb = rows // BLOCKS, d // NT, f // JT, d // XT
         hb, ib = rb // 2, xb // 2
         like = [jax.ShapeDtypeStruct(a.shape, a.dtype) for a in (x, w_gate, w_up, w_down)]
-        between = [jax.ShapeDtypeStruct((rows, f), BF)]
+        between = [jax.ShapeDtypeStruct((EARLY * jb, d), BF), jax.ShapeDtypeStruct((rows, f), BF)]
         between += [jax.ShapeDtypeStruct((UNITS, hb, cb), BF), jax.ShapeDtypeStruct((UNITS, hb, cb), F32)]
         dma, vm = pltpu.SemaphoreType.DMA, pltpu.VMEM
         hbm = pl.BlockSpec(memory_space=pl.ANY)
         scratch = [
-            vm((rows, f), BF), vm((rows, f), BF), vm((2, rb, jb), BF),
+            vm((rows, f), BF), vm((rows, f), BF), vm((rows, EARLY * jb), BF), vm((2, jb, xb), BF), vm((2, rb, jb), BF),
             vm((rb, d), BF), vm((2, jb, d), BF), vm((2, rb, jb), BF), vm((2, rb, jb), BF),
             vm((2, cb, f), BF), vm((2, cb, f), BF), vm((2, rows, xb), BF),
             vm((2, ib, f), BF), vm((2, ib, f), BF),
             vm((4, hb, cb), BF), vm((4, hb, cb), BF), vm((4, hb, cb), F32), vm((2, hb, cb), BF),
             vm((RING, hb, cb), BF), vm((RING, hb, cb), BF), vm((RING, hb, cb), BF), vm((4, hb, cb), BF), vm((2, hb, cb), F32),
-            dma(()), dma((2,)), dma((2,)), dma((2,)), dma((2,)), dma((2,)), dma((2,)), dma((2,)), dma((2,)), dma((2,)),
+            dma(()), dma((2,)), dma((2,)), dma((2,)), dma((2,)), dma((2,)), dma((2,)), dma((2,)), dma((2,)), dma((2,)), dma((2,)),
             dma((4,)), dma((4,)), dma((2,)), dma((2,)), dma((RING,)), dma((RING,)), dma((RING,)), dma((RING,)),
             dma((4,)), dma((UNITS,)), dma((4,)), dma((UNITS,)), dma((4,)),
         ]
-        dx, dwg, dwu, hid, *_ = pl.pallas_call(
+        dx, dwg, dwu, early, hid, *_ = pl.pallas_call(
             kernel,
             out_shape=like[:3] + between,
             in_specs=[hbm] * 7,
-            out_specs=[hbm] * 6,
+            out_specs=[hbm] * 7,
             scratch_shapes=scratch,
             compiler_params=pltpu.CompilerParams(
                 collective_id=0, has_side_effects=True, vmem_limit_bytes=67_000_000
@@ -517,16 +569,17 @@
             pl.pallas_call(
                 down_kernel,
                 out_shape=like,
-                in_specs=[hbm] * 5,
+                in_specs=[hbm] * 6,
                 out_specs=[hbm] * 4,
                 scratch_shapes=[
-                    vm((JT, rows, jb), BF), vm((2, rows, d // DT), BF), vm((2, jb, d // DT), BF),
+                    vm((JT - EARLY, rows, jb), BF), vm((2, rows, d // DT), BF), vm((2, jb, d // DT), BF),
                     vm((RING, rows // CHUNKS, d), BF), vm((RING, d // CHUNKS, f), BF), vm((RING, d // CHUNKS, f), BF),
-                    dma((JT,)), dma((2,)), dma((2,)), dma((3, RING)), dma((3, RING)),
+                    vm((RING, EARLY * jb // CHUNKS, d), BF),
+                    dma((JT - EARLY,)), dma((2,)), dma((2,)), dma((4, RING)), dma((4, RING)),
                 ],
                 compiler_params=pltpu.CompilerParams(vmem_limit_bytes=67_000_000),
                 name="mlp_down",
-            )(hid, dy, dx, dwg, dwu)
+            )(hid, dy, dx, dwg, dwu, early)
         )
 
     tokens, columns, rows = P("dp", None), P(None, "tp"), P("tp", None)

time: 340 us -> 357 us (1.050)
  Pallas kernels: 340 us -> 356 us
    pallas_call x1, Pallas kernels: 282 us -> 295 us  [step(): pl.pallas_call(kernel, out_shape=like[:3] + between, in_specs=[hbm] * 7,...]
    pallas_call x1, Pallas kernels: 57.2 us -> 61.6 us  [step(): pl.pallas_call(down_kernel, out_shape=like, in_specs=[hbm] * 6, out_specs...]
where the time goes in v3:
time: 357 us
  Pallas kernels  356 us (100%)
    pallas_call x1, Pallas kernels, step(): pl.pallas_call(kernel, out_shape=like[:3] + between, in_specs=[hbm] * 7,...  295 us
    pallas_call x1, Pallas kernels, step(): pl.pallas_call(down_kernel, out_shape=like, in_specs=[hbm] * 6, out_specs...  61.6 us

profile of v3, /device:TPU:0, one launch (start us, length us, event | category | flops | bytes accessed | tf_op | source)
XLA Modules:
  0.0 356.8 jit_solution(13646637955552390281)
XLA Ops:
  0.6 294.6 %mlp_backward.1 = (bf16[2048,5120]{1,0:T(8,128)(2,1)}, bf16[5120,1792]{1,0:T(8,128)(2,1)}, bf16[5120,1792]{1,0:T(8,128)(2,1)}, bf16[512,5120]{1,0:T(8,128)(2,1)}...) custom-call(bf16[2048,5120]{1,0:T(8,128)(2,1)} %x.1, bf16[2048,5120]{1,0:T(8,128)(2,1)} %dy.3, ...), custom_call_target="tpu_custom_call" | custom-call | tf_op jit(solution)/shard_map/mlp_backward/pallas_call | solution.py:557
  295.3 61.6 %mlp_down.1 = (bf16[2048,5120]{1,0:T(8,128)(2,1)}, bf16[5120,1792]{1,0:T(8,128)(2,1)}, bf16[5120,1792]{1,0:T(8,128)(2,1)}, bf16[1792,5120]{1,0:T(8,128)(2,1)}) custom-call(bf16[2048,1792]{1,0:T(8,128)(2,1)} %get-tuple-element.9.hid, bf16[2048,5120]{1,0:T(8,128)(2,1)} %dy.3, bf16[2048,5120]{1,0:T(8,128)(2,1)} %get-tuple-element.10.dx, ...), custom_call_target="tpu_custom_call" | custom-call | tf_op jit(solution)/shard_map/mlp_down/pallas_call | solution.py:569
